TPU v7x, 512 devices: a whole 4x4x16 slice. The times are simulated.
512 devices in a mesh: tile: 16 (over y, x), depth: 32 (over z, core).
Axes of the slice: x: 4, y: 4, z: 16, core: 2. Of those that a mesh axis runs over, the one named last changes fastest.
Arguments:
- patches: float32 [1024, 256, 256], P('tile', 'depth'), may hold values from -6 to 6
- patch_owner: int32 [1024, 1], P('tile'), may hold values from 0 to 15; in each aligned block of 64 rows (0 to 63, 64 to 127, ...) at most 8 rows name the same one
- patch_level: int32 [1024], P('tile'), may hold values from 0 to 63
- phases: float32 [1024, 256, 256], P('tile', None, 'depth'), may hold values from -3.140625 to 3.140625
Outputs:
- intensity: float32 [1024, 256, 256], P('tile', 'depth')
Inputs may be any that keep to these rules, and one draw needn't show every extreme that they name: `patch_owner`: among the 64 patches of one index of tile, at most 8 have the same owner.
All inputs are finite; a program needn't handle non-finite values.
Results may differ from a plain program's by a relative error of at most 0.00017.
Values sent between devices are 32-bit elements; how exact they have to be, the bound alone decides.
A program may use at most 64 MiB of HBM per device.

v0:
```python
import math

import jax
import jax.numpy as jnp
from jax import lax
from jax.sharding import PartitionSpec as P

HIGHEST_PRECISION = lax.Precision.HIGHEST


def sent_together(arrays, axis, split_dim, concat_dim, along):
    widths = [a.shape[along] for a in arrays]
    both = jnp.concatenate(arrays, axis=along)
    filled = lax.all_to_all(both, axis, split_axis=split_dim, concat_axis=concat_dim, tiled=True)
    return tuple(jnp.split(filled, [sum(widths[:k]) for k in range(1, len(widths))], axis=along))


def tables(extent):
    indices = jnp.arange(extent, dtype=jnp.int32)
    product = indices[:, None] * indices[None, :] % extent
    angles = product.astype(jnp.float32) * (2.0 * math.pi / extent)
    return (jnp.cos(angles), jnp.sin(angles))


def right_apply(values, matrix):
    return jnp.einsum(
        "src,ck->srk",
        values,
        matrix,
        precision=HIGHEST_PRECISION,
        preferred_element_type=jnp.float32,
    )


def apply_rows(matrix, values):
    return jnp.einsum(
        "jk,skc->sjc",
        matrix,
        values,
        precision=HIGHEST_PRECISION,
        preferred_element_type=jnp.float32,
    )


def refocus(field, real_gain, imag_gain):
    extent = field.shape[2]
    cosine_table, sine_table = tables(extent)
    col_real = right_apply(field, cosine_table)
    col_imag = -right_apply(field, sine_table)
    col_real, col_imag = sent_together((col_real, col_imag), "depth", 2, 1, 0)
    spec_real = apply_rows(cosine_table, col_real) + apply_rows(sine_table, col_imag)
    spec_imag = apply_rows(cosine_table, col_imag) - apply_rows(sine_table, col_real)
    prop_real = spec_real * real_gain - spec_imag * imag_gain
    prop_imag = spec_real * imag_gain + spec_imag * real_gain
    back_real = apply_rows(cosine_table, prop_real) - apply_rows(sine_table, prop_imag)
    back_imag = apply_rows(cosine_table, prop_imag) + apply_rows(sine_table, prop_real)
    back_real, back_imag = sent_together((back_real, back_imag), "depth", 1, 2, 0)
    field_real = right_apply(back_real, cosine_table) - right_apply(back_imag, sine_table)
    field_imag = right_apply(back_real, sine_table) + right_apply(back_imag, cosine_table)
    return (field_real * field_real + field_imag * field_imag) * (1.0 / float(extent) ** 4)


def select_gains(selector, phase_block, lead):
    flattened = phase_block.reshape(phase_block.shape[0], -1)
    real_gain = jnp.dot(
        selector,
        jnp.cos(flattened),
        precision=HIGHEST_PRECISION,
        preferred_element_type=jnp.float32,
    )
    imag_gain = jnp.dot(
        selector,
        jnp.sin(flattened),
        precision=HIGHEST_PRECISION,
        preferred_element_type=jnp.float32,
    )
    shape_out = (lead, phase_block.shape[1], phase_block.shape[2])
    return (real_gain.reshape(shape_out), imag_gain.reshape(shape_out))


def on_device(patches, patch_owner, patch_level, phases):
    patch_count, row_count, extent = patches.shape
    levels = phases.shape[0]
    owners = lax.axis_size("tile")
    owner_column = patch_owner[:, 0]
    gathered = lax.all_gather(phases, "tile", axis=0, tiled=True)
    depth_index = owner_column * levels + patch_level
    depth_hot = (
        depth_index[:, None] == jnp.arange(owners * levels, dtype=jnp.int32)[None, :]
    ).astype(jnp.float32)
    real_gain, imag_gain = select_gains(depth_hot, gathered, patch_count)
    return refocus(patches, real_gain, imag_gain)


def solution(mesh):
    return jax.shard_map(
        on_device,
        mesh=mesh,
        in_specs=(P("tile", "depth", None), P("tile", None), P("tile"), P("tile", None, "depth")),
        out_specs=P("tile", "depth", None),
        check_vma=False,
    )
```

profile of v0, /device:TPU:1, one launch (start us, length us, event | category | flops | bytes accessed | tf_op | source)
XLA Modules:
  0.0 253.2 jit_solution(1416911551636459273)
XLA Ops:
  6.5 0.0 copy-start
  6.5 0.0 copy-start.2
  6.5 0.0 copy-start.3
  6.5 0.0 all-gather.2.cloned.1.call-start
  6.5 0.7 all-gather.2.cloned.1.call-update
  7.3 0.3 copy-done
  7.6 1.6 fusion.4
  9.2 1.6 convolution_bitcast_fusion
  10.8 0.1 pad_maximum_fusion
  10.9 1.4 copy.66
  12.3 17.3 %all-to-all-start = ((f32[128,8,256]{0,1,2:T(8,128)}), f32[128,8,256]{0,1,2:T(8,128)S(1)}, u32[]{:S(2)}, u32[]{:S(2)}) async-start(f32[128,8,256]{0,1,2:T(8,128)} %copy.66), calls=%async_computation | async-start | bytes 2097152 | tf_op jit(solution)/shard_map/all_to_all | solution.py:14
  29.6 0.0 copy-done.2
  29.6 0.0 copy-done.3
  29.7 55.5 %all-to-all-done = f32[128,8,256]{0,1,2:T(8,128)S(1)} async-done(((f32[128,8,256]{0,1,2:T(8,128)}), f32[128,8,256]{0,1,2:T(8,128)S(1)}, u32[]{:S(2)}, u32[]{:S(2)}) %all-to-all-start) | async-done | bytes 1048608 | tf_op jit(solution)/shard_map/all_to_all | solution.py:14
  85.2 0.2 copy.104
  85.4 0.3 fusion.119
  85.8 0.1 copy.68
  85.9 0.5 copy.69
  86.4 0.1 copy.70
  86.5 0.5 copy.71
  86.9 1.6 fusion.35
  88.5 2.4 fusion.33
  90.9 1.6 fusion.12
  92.4 9.2 %all-gather.2.cloned.1.call-done = f32[1024,256,8]{1,2,0:T(8,128)} async-done(((f32[64,256,8]{1,2,0:T(8,128)}), f32[1024,256,8]{1,2,0:T(8,128)}) %all-gather.2.cloned.1.call-update) | async-done | bytes 8388624 | tf_op jit(solution)/shard_map/all_gather | solution.py:86
  101.7 8.8 %copy.72 = f32[1024,256,8]{0,2,1:T(8,128)} copy(f32[1024,256,8]{1,2,0:T(8,128)} %all-gather.2.cloned.1.call-done) | data formatting | bytes 16777216 | tf_op jit(solution)/shard_map/all_gather | solution.py:86
  110.5 30.3 %cosine_bitcast_fusion = (f32[256,8,1024]{2,1,0:T(8,128)S(1)}, f32[256,8,1024]{2,1,0:T(8,128)S(1)}) fusion(f32[1024,256,8]{0,2,1:T(8,128)} %copy.72), kind=kLoop, calls=%fused_computation.5 | loop fusion | bytes 25165824 | tf_op jit(solution)/shard_map/dot_general | solution.py:65
  140.8 0.0 copy-start.1
  140.8 9.3 %fusion.2 = f32[64,256,8]{1,0,2:T(8,128)S(1)} fusion(f32[256,8,1024]{2,1,0:T(8,128)S(1)} %get-tuple-element.5, s32[64]{0:T(128)S(1)} %bitcast_add_fusion), kind=kOutput, calls=%fused_computation.2 | convolution fusion | flops 1610678272 | bytes 8913152 | tf_op jit(solution)/shard_map/dot_general | solution.py:65
  150.1 9.5 %fusion = f32[64,256,8]{1,0,2:T(8,128)S(1)} fusion(f32[256,8,1024]{2,1,0:T(8,128)S(1)} %get-tuple-element.6, s32[64]{0:T(128)S(1)} %bitcast_add_fusion), kind=kOutput, calls=%fused_computation | convolution fusion | flops 1610678272 | bytes 8913152 | tf_op jit(solution)/shard_map/dot_general | solution.py:71
  159.6 0.0 copy-done.1
  159.6 2.0 multiply_subtract_fusion
  161.7 1.6 fusion.31
  163.2 1.6 fusion.29
  164.8 1.8 fusion.10
  166.6 1.6 fusion.9
  168.2 0.1 pad_maximum_fusion.1
  168.3 0.6 copy.82
  168.8 68.6 %all_to_all.30 = f32[128,256,8]{0,2,1:T(8,128)S(1)} all-to-all(f32[128,256,8]{0,2,1:T(8,128)S(1)} %copy.82), channel_id=1, replica_groups=mesh['tile'=16,'depth'=32] {'depth'}, dimensions={1} | all-to-all | bytes 2097152 | tf_op jit(solution)/shard_map/all_to_all | solution.py:14
  237.5 0.4 fusion.118
  237.9 0.2 copy_bitcast_fusion
  238.1 0.4 copy.84
  238.5 1.6 fusion.18
  240.0 1.6 fusion.27
  241.6 0.4 copy.86
  242.0 1.6 fusion.8
  243.6 2.4 fusion.7
  (1 shorter events, 0.0 us)
Async XLA Ops:
  6.5 1.0 copy-start
  6.5 23.1 %copy-start.2 = (s32[64]{0:T(128)S(1)}, s32[64]{0:T(128)}, u32[]{:S(2)}) copy-start(s32[64]{0:T(128)} %param.6) | copy-start | bytes 772
  6.5 23.1 %copy-start.3 = (s32[64,1]{0,1:T(1,128)S(1)}, s32[64,1]{0,1:T(1,128)}, u32[]{:S(2)}) copy-start(s32[64,1]{0,1:T(1,128)} %param.5) | copy-start | bytes 772
  6.5 95.1 %all-gather.2.cloned.1.call-start = ((), (), s32[]{:S(2)}) async-start(), calls=%async_computation.2 | async-start | bytes 8912896 | tf_op jit(solution)/shard_map/all_gather | solution.py:86
  12.3 72.9 %all-to-all-start = ((f32[128,8,256]{0,1,2:T(8,128)}), f32[128,8,256]{0,1,2:T(8,128)S(1)}, u32[]{:S(2)}, u32[]{:S(2)}) async-start(f32[128,8,256]{0,1,2:T(8,128)} %copy.66), calls=%async_computation | async-start | bytes 2097152 | tf_op jit(solution)/shard_map/all_to_all | solution.py:14
  140.8 18.9 %copy-start.1 = (f32[64,8,256]{2,1,0:T(8,128)S(1)}, f32[64,8,256]{2,1,0:T(8,128)}, u32[]{:S(2)}) copy-start(f32[64,8,256]{2,1,0:T(8,128)} %fusion.33) | copy-start | bytes 1572868
Sparse Core Ops, SparseCore 0:
  10.3 91.2 all-gather.1
where the time goes:
time: 257 us; the launch traced here: 253 us
  blocking collectives  68.6 us (27%)
  waiting for transfers between devices  65.5 us (25%)
  local copies, waits for them, and re-layouts  44.4 us (17%)
  matrix products  43.1 us (17%)
  starting transfers between devices  17.3 us (7%)
  between operations  14.1 us (5%)
    all_to_all x1, blocking collectives, sent_together(): lax.all_to_all(both, axis, split_axis=split_dim, concat_axis=concat_dim,...  68.6 us
    all_to_all x1, waiting for transfers between devices, sent_together(): lax.all_to_all(both, axis, split_axis=split_dim, concat_axis=concat_dim,...  55.5 us
    dot_general x1, local copies, waits for them, and re-layouts, select_gains(): jnp.dot(selector, jnp.cos(flattened), precision=HIGHEST_PRECISION, prefer...  30.3 us
    all_to_all x1, starting transfers between devices, sent_together(): lax.all_to_all(both, axis, split_axis=split_dim, concat_axis=concat_dim,...  17.3 us
    dot_general x8, matrix products, apply_rows(): jnp.einsum('jk,skc->sjc', matrix, values, precision=HIGHEST_PRECISION, pr...  14 us
    dot_general x6, matrix products, right_apply(): jnp.einsum('src,ck->srk', values, matrix, precision=HIGHEST_PRECISION, pr...  10.3 us
    dot_general x1, matrix products, select_gains(): jnp.dot(selector, jnp.sin(flattened), precision=HIGHEST_PRECISION, prefer...  9.53 us
    dot_general x1, matrix products, select_gains(): jnp.dot(selector, jnp.cos(flattened), precision=HIGHEST_PRECISION, prefer...  9.32 us
  transfers between devices with their start and end apart: 2, of which 2 were waited for; matrix products, arithmetic and copies ran while one was open for 5% of the time, Pallas kernels for 0%

commit v1 on v0

v1 whole, which is shorter than its diff:
```python
import functools
import math

import jax
import jax.numpy as jnp
import numpy as np
from jax import lax
from jax.experimental import pallas as pl
from jax.experimental.pallas import tpu as pltpu
from jax.sharding import PartitionSpec as P

CAP = 8
LANES = 128


def dft_tables(extent):
    indices = np.arange(extent)
    angles = (indices[:, None] * indices[None, :] % extent) * (2.0 * math.pi / extent)
    exact = np.concatenate([np.cos(angles), np.sin(angles)], axis=0)
    high = exact.astype(np.float32).astype(jnp.bfloat16)
    low = (exact - high.astype(np.float64)).astype(np.float32).astype(jnp.bfloat16)
    return np.concatenate([high, low, high], axis=1)


def split(values):
    high = values.astype(jnp.bfloat16)
    low = (values - high.astype(jnp.float32)).astype(jnp.bfloat16)
    return high, low


def apply_left(table, values):
    high, low = split(values)
    stacked = jnp.concatenate([high, high, low], axis=0)
    return jnp.dot(table, stacked, preferred_element_type=jnp.float32)


def apply_left_transposed(table, values):
    high, low = split(values)
    stacked = jnp.concatenate([high, high, low], axis=1)
    return lax.dot_general(table, stacked, (((1,), (1,)), ((), ())), preferred_element_type=jnp.float32)


def polynomial(square, terms):
    total = jnp.full_like(square, terms[-1])
    for term in terms[-2::-1]:
        total = total * square + term
    return total


SIN_TERMS = [(-1.0) ** n / math.factorial(2 * n + 1) for n in range(7)]
COS_TERMS = [(-1.0) ** n / math.factorial(2 * n) for n in range(8)]


def cos_sin(phase):
    half = phase * 0.5
    square = half * half
    sine = half * polynomial(square, SIN_TERMS)
    cosine = polynomial(square, COS_TERMS)
    return 1.0 - 2.0 * sine * sine, 2.0 * sine * cosine


def far_first(step, extent):
    return extent // 2 + (step // 2) * (1 - 2 * (step % 2)) - step % 2


def kernel(
    tiles,
    patches,
    owner,
    level,
    phases,
    tables,
    out,
    table,
    depths,
    slot_row,
    slot_at,
    want_row,
    wants,
    wants_at,
    packed,
    got,
    chosen,
    pixels,
    phase,
    spectrum,
    intensity,
    local_sem,
    want_send,
    want_recv,
    pack_send,
    pack_recv,
    pixel_send,
    pixel_recv,
    phase_send,
    phase_recv,
    out_send,
    out_recv,
):
    count, rows, extent = patches.shape
    spread = extent // rows
    ring = spread // 2
    own = count // spread
    side = math.isqrt(tiles)
    me_t, me_d = lax.axis_index("tile"), lax.axis_index("depth")
    me_y, me_x, me_z, me_c = me_t // side, me_t % side, me_d // 2, me_d % 2

    def depth_pair(step):
        hop, swap = far_first(step // 2, ring), 1 - step % 2
        to = ((me_z + hop) % ring) * 2 + (me_c + swap) % 2
        source = ((me_z + ring - hop) % ring) * 2 + (me_c + swap) % 2
        return to, source

    def tile_pair(step):
        down, over = far_first(step // side, side), far_first(step % side, side)
        to = ((me_y + down) % side) * side + (me_x + over) % side
        source = ((me_y + side - down) % side) * side + (me_x + side - over) % side
        return to, source

    depth_steps, tile_steps = spread - 1, tiles - 1

    barrier = pltpu.get_barrier_semaphore()

    @pl.loop(0, depth_steps)
    def _(step):
        pl.semaphore_signal(barrier, inc=1, device_id={"depth": depth_pair(step)[0]})

    @pl.loop(0, tile_steps)
    def _(step):
        pl.semaphore_signal(barrier, inc=1, device_id={"tile": tile_pair(step)[0]})

    load_depths = pltpu.make_async_copy(phases, depths, local_sem.at[0])
    load_depths.start()
    load_table = pltpu.make_async_copy(tables, table, local_sem.at[1])
    load_table.start()
    load_pixels = pltpu.make_async_copy(
        patches.at[pl.ds(me_d * own, own)], pixels.at[:, pl.ds(me_d * rows, rows), :], local_sem.at[2]
    )
    load_pixels.start()

    lane = lax.broadcasted_iota(jnp.int32, (1, LANES), 1)
    owners = lax.fori_loop(
        0, count, lambda p, row: jnp.where(lane == p, owner[0, p], row), jnp.full((1, LANES), -1, jnp.int32)
    )
    ranks = lax.fori_loop(
        0,
        count,
        lambda p, row: row + jnp.where((owners == owner[0, p]) & (lane > p), 1, 0),
        jnp.zeros((1, LANES), jnp.int32),
    )
    slot_row[...] = owners * CAP + ranks
    load_slots = pltpu.make_async_copy(slot_row, slot_at, local_sem.at[3])
    load_slots.start()
    load_slots.wait()
    wanted = lax.fori_loop(
        0,
        count,
        lambda p, row: jnp.where(lane == slot_at[0, p], level[0, p], row),
        jnp.zeros((1, LANES), jnp.int32),
    )
    want_row[...] = wanted
    wants[me_t] = wanted

    pl.semaphore_wait(barrier, depth_steps + tile_steps)

    def want_copy(step, to, source):
        return pltpu.make_async_remote_copy(
            src_ref=want_row,
            dst_ref=wants.at[source],
            send_sem=want_send.at[step],
            recv_sem=want_recv.at[step],
            device_id={"tile": to},
        )

    def pixel_copy(step, to, source):
        return pltpu.make_async_remote_copy(
            src_ref=patches.at[pl.ds(to * own, own)],
            dst_ref=pixels.at[:, pl.ds(source * rows, rows), :],
            send_sem=pixel_send.at[step],
            recv_sem=pixel_recv.at[step],
            device_id={"depth": to},
        )

    def pack_copy(step, to, source):
        return pltpu.make_async_remote_copy(
            src_ref=packed.at[to],
            dst_ref=got.at[pl.ds(source * CAP, CAP)],
            send_sem=pack_send.at[step],
            recv_sem=pack_recv.at[step],
            device_id={"tile": to},
        )

    def phase_copy(which, step, to, source):
        return pltpu.make_async_remote_copy(
            src_ref=chosen.at[which, to],
            dst_ref=phase.at[which, pl.ds(source * rows, rows), :],
            send_sem=phase_send.at[which, step],
            recv_sem=phase_recv.at[which, step],
            device_id={"depth": to},
        )

    def out_copy(which, step, to, source):
        return pltpu.make_async_remote_copy(
            src_ref=intensity.at[which, pl.ds(to * rows, rows), :],
            dst_ref=out.at[source * own + which],
            send_sem=out_send.at[which, step],
            recv_sem=out_recv.at[which, step],
            device_id={"depth": to},
        )

    @pl.loop(0, tile_steps)
    def _(step):
        want_copy(step, tile_pair(step)[0], me_t).start()

    @pl.loop(0, depth_steps)
    def _(step):
        pixel_copy(step, depth_pair(step)[0], me_d).start()

    load_depths.wait()

    @pl.loop(0, tile_steps)
    def _(step):
        to, source = tile_pair(step)
        want_copy(step, to, source).wait_recv()

    load_wants = pltpu.make_async_copy(wants, wants_at, local_sem.at[3])
    load_wants.start()
    load_wants.wait()

    @pl.loop(0, tile_steps)
    def _(step):
        to = tile_pair(step)[0]
        for slot in range(CAP):
            packed[to, slot] = depths[wants_at[to, 0, me_t * CAP + slot]]
        pack_copy(step, to, me_t).start()

    for slot in range(CAP):
        got[me_t * CAP + slot] = depths[wants_at[me_t, 0, me_t * CAP + slot]]

    @pl.loop(0, tile_steps)
    def _(step):
        to, source = tile_pair(step)
        pack_copy(step, to, source).wait_recv()

    @pl.loop(0, own)
    def _(which):
        @pl.loop(0, depth_steps)
        def _(step):
            to = depth_pair(step)[0]
            chosen[which, to] = got[slot_at[0, to * own + which]]
            phase_copy(which, step, to, me_d).start()

        phase[which, pl.ds(me_d * rows, rows), :] = got[slot_at[0, me_d * own + which]]

    load_table.wait()
    load_pixels.wait()

    @pl.loop(0, depth_steps)
    def _(step):
        to, source = depth_pair(step)
        pixel_copy(step, to, source).wait_recv()

    @pl.loop(0, own)
    def _(which):
        columns = apply_left(table[...], pixels[which])
        both = apply_left_transposed(table[...], columns)
        spectrum[which, 0] = both[:extent, :extent] - both[extent:, extent:]
        spectrum[which, 1] = -(both[:extent, extent:] + both[extent:, :extent])

    @pl.loop(0, own)
    def _(which):
        @pl.loop(0, depth_steps)
        def _(step):
            to, source = depth_pair(step)
            phase_copy(which, step, to, source).wait_recv()

        cosine, sine = cos_sin(phase[which])
        scale = 1.0 / float(extent * extent)
        real, imag = spectrum[which, 0] * scale, spectrum[which, 1] * scale
        moved = jnp.concatenate([real * cosine - imag * sine, real * sine + imag * cosine], axis=1)
        both = apply_left(table[...], moved)
        back = jnp.concatenate(
            [both[:extent, :extent] - both[extent:, extent:], both[:extent, extent:] + both[extent:, :extent]], axis=0
        )
        both = apply_left_transposed(table[...], back)
        field_real = both[:extent, :extent] - both[extent:, extent:]
        field_imag = both[:extent, extent:] + both[extent:, :extent]
        intensity[which] = field_real * field_real + field_imag * field_imag

        @pl.loop(0, depth_steps)
        def _(step):
            out_copy(which, step, depth_pair(step)[0], me_d).start()

        pltpu.make_async_copy(
            intensity.at[which, pl.ds(me_d * rows, rows), :], out.at[me_d * own + which], local_sem.at[4 + which]
        ).start()

    @pl.loop(0, tile_steps)
    def _(step):
        to, source = tile_pair(step)
        want_copy(step, to, source).wait_send()
        pack_copy(step, to, source).wait_send()

    @pl.loop(0, depth_steps)
    def _(step):
        to, source = depth_pair(step)
        pixel_copy(step, to, source).wait_send()

    @pl.loop(0, own)
    def _(which):
        @pl.loop(0, depth_steps)
        def _(step):
            to, source = depth_pair(step)
            phase_copy(which, step, to, source).wait_send()
            out_copy(which, step, to, source).wait()

        pltpu.make_async_copy(
            intensity.at[which, pl.ds(me_d * rows, rows), :], out.at[me_d * own + which], local_sem.at[4 + which]
        ).wait()


def solution(mesh):
    tiles, spread = mesh.shape["tile"], mesh.shape["depth"]

    def on_device(patches, patch_owner, patch_level, phases):
        count, rows, extent = patches.shape
        own = count // spread
        depth_count = phases.shape[0]
        tables = jnp.asarray(dft_tables(extent))
        any_space = pl.BlockSpec(memory_space=pl.ANY)
        scalars = pl.BlockSpec(memory_space=pltpu.SMEM)
        f32, dma = jnp.float32, pltpu.SemaphoreType.DMA
        return pl.pallas_call(
            functools.partial(kernel, tiles),
            out_shape=jax.ShapeDtypeStruct(patches.shape, patches.dtype),
            in_specs=[any_space, scalars, scalars, any_space, any_space],
            out_specs=any_space,
            scratch_shapes=[
                pltpu.VMEM(tables.shape, tables.dtype),
                pltpu.VMEM((depth_count, rows, extent), f32),
                pltpu.VMEM((1, LANES), jnp.int32),
                pltpu.SMEM((1, LANES), jnp.int32),
                pltpu.VMEM((1, LANES), jnp.int32),
                pltpu.VMEM((tiles, 1, LANES), jnp.int32),
                pltpu.SMEM((tiles, 1, LANES), jnp.int32),
                pltpu.VMEM((tiles, CAP, rows, extent), f32),
                pltpu.VMEM((tiles * CAP, rows, extent), f32),
                pltpu.VMEM((own, spread, rows, extent), f32),
                pltpu.VMEM((own, extent, extent), f32),
                pltpu.VMEM((own, extent, extent), f32),
                pltpu.VMEM((own, 2, extent, extent), f32),
                pltpu.VMEM((own, extent, extent), f32),
                dma((4 + own,)),
                dma((tiles,)),
                dma((tiles,)),
                dma((tiles,)),
                dma((tiles,)),
                dma((spread,)),
                dma((spread,)),
                dma((own, spread)),
                dma((own, spread)),
                dma((own, spread)),
                dma((own, spread)),
            ],
            compiler_params=pltpu.CompilerParams(
                collective_id=0, has_side_effects=True, vmem_limit_bytes=60 * 1024 * 1024
            ),
        )(
            patches,
            patch_owner.reshape(1, count),
            patch_level.reshape(1, count),
            jnp.transpose(phases, (0, 2, 1)),
            tables,
        )

    return jax.shard_map(
        on_device,
        mesh=mesh,
        in_specs=(P("tile", "depth", None), P("tile", None), P("tile"), P("tile", None, "depth")),
        out_specs=P("tile", "depth", None),
        check_vma=False,
    )
```

time: 257 us -> 92.7 us (0.36); the launches traced: 253 us -> 92.5 us
  Pallas kernels: 0 us -> 90.6 us
  blocking collectives: 68.6 us -> 0 us
  waiting for transfers between devices: 65.5 us -> 0 us
  matrix products: 43.1 us -> 0 us
  local copies, waits for them, and re-layouts: 44.4 us -> 1.87 us
  starting transfers between devices: 17.3 us -> 0 us
  between operations: 14.1 us -> 0.01 us
    pallas_call x0 -> x1, Pallas kernels: none -> 90.6 us  [on_device(): pl.pallas_call(functools.partial(kernel, tiles), out_shape=jax.ShapeDtype...]
    all_to_all x1 -> x0, blocking collectives: 68.6 us -> none  [sent_together(): lax.all_to_all(both, axis, split_axis=split_dim, concat_axis=concat_dim,...]
    all_to_all x1 -> x0, waiting for transfers between devices: 55.5 us -> none  [sent_together(): lax.all_to_all(both, axis, split_axis=split_dim, concat_axis=concat_dim,...]
    dot_general x16 -> x0, matrix products: 43.1 us -> none  [the longest x8 14 us: apply_rows(): jnp.einsum('jk,skc->sjc', matrix, values, precision=HIGHEST_PRECISION, pr...]
    dot_general x1 -> x0, local copies, waits for them, and re-layouts: 30.3 us -> none  [select_gains(): jnp.dot(selector, jnp.cos(flattened), precision=HIGHEST_PRECISION, prefer...]
    all_to_all x1 -> x0, starting transfers between devices: 17.3 us -> none  [sent_together(): lax.all_to_all(both, axis, split_axis=split_dim, concat_axis=concat_dim,...]
    all_gather x1 -> x0, waiting for transfers between devices: 9.25 us -> none  [on_device(): gathered = lax.all_gather(phases, 'tile', axis=0, tiled=True)]
    all_gather x1 -> x0, local copies, waits for them, and re-layouts: 8.79 us -> none  [on_device(): gathered = lax.all_gather(phases, 'tile', axis=0, tiled=True)]
  transfers between devices with their start and end apart: 2 -> 0, of which waited for: 2 -> 0; matrix products, arithmetic and copies ran while one was open for 5% -> 0% of each run, Pallas kernels for 0% -> 0%
where the time goes in v1:
time: 92.7 us; the launch traced here: 92.5 us
  Pallas kernels  90.6 us (98%)
  local copies, waits for them, and re-layouts  1.87 us (2%)
    pallas_call x1, Pallas kernels, on_device(): pl.pallas_call(functools.partial(kernel, tiles), out_shape=jax.ShapeDtype...  90.6 us
    unnamed x1, local copies, waits for them, and re-layouts  1.87 us

profile of v1, /device:TPU:1, one launch (start us, length us, event | category | flops | bytes accessed | tf_op | source)
XLA Modules:
  0.0 92.5 jit_solution(8891894093114204733)
XLA Ops:
  0.0 90.6 %shard_map.55 = f32[64,8,256]{2,1,0:T(8,128)} custom-call(f32[64,8,256]{2,1,0:T(8,128)} %patches.1, s32[1,64]{1,0:T(1,128)} %bitcast.4, s32[1,64]{1,0:T(1,128)} %bitcast.5, f32[64,8,256]{2,1,0:T(8,128)} %bitcast.3, bf16[512,768]{1,0:T(8,128)(2,1)} %constant.2.clone.tables), custom_call_target="tpu_custom_call" | custom-call | tf_op jit(solution)/shard_map/pallas_call | solution.py:333
  90.6 1.9 %copy.7 = f32[64,8,256]{2,1,0:T(8,128)} copy(f32[64,8,256]{2,1,0:T(8,128)} %shard_map.55) | data formatting | bytes 1048576

commit v2 on v1

--- a/solution.py
+++ b/solution.py
@@ -11,6 +11,7 @@
 
 CAP = 8
 LANES = 128
+EDGES = (0, 1, 2, 3, 4, 8)
 
 
 def dft_tables(extent):
@@ -59,8 +60,14 @@
     return 1.0 - 2.0 * sine * sine, 2.0 * sine * cosine
 
 
-def far_first(step, extent):
-    return extent // 2 + (step // 2) * (1 - 2 * (step % 2)) - step % 2
+def near_first(step):
+    return ((step + 1) // 2) * (2 * (step % 2) - 1)
+
+
+def reaches(spread):
+    half = spread // 4
+    reach = max(1, half // 4)
+    return reach, -(-(half - reach) // reach)
 
 
 def kernel(
@@ -85,7 +92,10 @@
     phase,
     spectrum,
     intensity,
+    ring_sem,
     local_sem,
+    row_send,
+    row_recv,
     want_send,
     want_recv,
     pack_send,
@@ -105,29 +115,44 @@
     me_t, me_d = lax.axis_index("tile"), lax.axis_index("depth")
     me_y, me_x, me_z, me_c = me_t // side, me_t % side, me_d // 2, me_d % 2
 
-    def depth_pair(step):
-        hop, swap = far_first(step // 2, ring), 1 - step % 2
-        to = ((me_z + hop) % ring) * 2 + (me_c + swap) % 2
+    def peer(step):
+        hop, swap = near_first(step // 2), step % 2
+        to = ((me_z + ring + hop) % ring) * 2 + (me_c + swap) % 2
         source = ((me_z + ring - hop) % ring) * 2 + (me_c + swap) % 2
         return to, source
 
-    def tile_pair(step):
-        down, over = far_first(step // side, side), far_first(step % side, side)
+    def shifted(down, over):
         to = ((me_y + down) % side) * side + (me_x + over) % side
         source = ((me_y + side - down) % side) * side + (me_x + side - over) % side
         return to, source
 
-    depth_steps, tile_steps = spread - 1, tiles - 1
+    reach, ring_rounds = reaches(spread)
+
+    def within(distance):
+        return min(2 * (2 * distance + 1), spread)
 
     barrier = pltpu.get_barrier_semaphore()
 
-    @pl.loop(0, depth_steps)
+    @pl.loop(1, within(reach))
     def _(step):
-        pl.semaphore_signal(barrier, inc=1, device_id={"depth": depth_pair(step)[0]})
-
-    @pl.loop(0, tile_steps)
-    def _(step):
-        pl.semaphore_signal(barrier, inc=1, device_id={"tile": tile_pair(step)[0]})
+        pl.semaphore_signal(barrier, inc=1, device_id={"depth": peer(step)[0]})
+
+    @pl.loop(1, side)
+    def _(shift):
+        pl.semaphore_signal(barrier, inc=1, device_id={"tile": shifted(0, shift)[0]})
+        pl.semaphore_signal(barrier, inc=1, device_id={"tile": shifted(shift, 0)[0]})
+
+    def tell_ring(turn):
+        for way, hop in enumerate((reach, ring - reach)):
+            to = ((me_z + hop) % ring) * 2 + me_c
+            pl.semaphore_signal(ring_sem.at[turn, way], inc=1, device_id={"depth": to})
+
+    def learn_ring(turn):
+        for way in range(2):
+            pl.semaphore_wait(ring_sem.at[turn, way], 1)
+        if turn + 1 < ring_rounds:
+            tell_ring(turn + 1)
+        send_pixels(turn + 1)
 
     load_depths = pltpu.make_async_copy(phases, depths, local_sem.at[0])
     load_depths.start()
@@ -161,15 +186,25 @@
     want_row[...] = wanted
     wants[me_t] = wanted
 
-    pl.semaphore_wait(barrier, depth_steps + tile_steps)
-
-    def want_copy(step, to, source):
+    pl.semaphore_wait(barrier, within(reach) - 1 + 2 * (side - 1))
+    tell_ring(0)
+
+    def row_copy(shift, source):
         return pltpu.make_async_remote_copy(
             src_ref=want_row,
             dst_ref=wants.at[source],
-            send_sem=want_send.at[step],
-            recv_sem=want_recv.at[step],
-            device_id={"tile": to},
+            send_sem=row_send.at[shift],
+            recv_sem=row_recv.at[shift],
+            device_id={"tile": shifted(0, shift)[0]},
+        )
+
+    def want_copy(shift, source_row):
+        return pltpu.make_async_remote_copy(
+            src_ref=wants.at[pl.ds(me_y * side, side)],
+            dst_ref=wants.at[pl.ds(source_row * side, side)],
+            send_sem=want_send.at[shift],
+            recv_sem=want_recv.at[shift],
+            device_id={"tile": shifted(shift, 0)[0]},
         )
 
     def pixel_copy(step, to, source):
@@ -208,45 +243,74 @@
             device_id={"depth": to},
         )
 
-    @pl.loop(0, tile_steps)
-    def _(step):
-        want_copy(step, tile_pair(step)[0], me_t).start()
-
-    @pl.loop(0, depth_steps)
-    def _(step):
-        pixel_copy(step, depth_pair(step)[0], me_d).start()
-
-    load_depths.wait()
-
-    @pl.loop(0, tile_steps)
-    def _(step):
-        to, source = tile_pair(step)
-        want_copy(step, to, source).wait_recv()
-
-    load_wants = pltpu.make_async_copy(wants, wants_at, local_sem.at[3])
-    load_wants.start()
-    load_wants.wait()
-
-    @pl.loop(0, tile_steps)
-    def _(step):
-        to = tile_pair(step)[0]
+    def send_pixels(turn):
+        first = 1 if turn == 0 else within(turn * reach)
+
+        @pl.loop(first, within((turn + 1) * reach))
+        def _(step):
+            pixel_copy(step, peer(step)[0], me_d).start()
+
+    def send_packed(down, over):
+        to = shifted(down, over)[0]
         for slot in range(CAP):
             packed[to, slot] = depths[wants_at[to, 0, me_t * CAP + slot]]
-        pack_copy(step, to, me_t).start()
+        pack_copy(down * side + over, to, me_t).start()
+
+    def read_wants(row):
+        load = pltpu.make_async_copy(
+            wants.at[pl.ds(row * side, side)], wants_at.at[pl.ds(row * side, side)], local_sem.at[3]
+        )
+        load.start()
+        load.wait()
+
+    @pl.loop(1, side)
+    def _(shift):
+        row_copy(shift, me_t).start()
+
+    send_pixels(0)
+    learn_ring(0)
+
+    @pl.loop(1, side)
+    def _(shift):
+        row_copy(shift, shifted(0, shift)[1]).wait_recv()
+
+    @pl.loop(1, side)
+    def _(shift):
+        want_copy(shift, me_y).start()
+
+    for turn in range(1, ring_rounds):
+        learn_ring(turn)
+    load_depths.wait()
+    read_wants(me_y)
+
+    @pl.loop(1, side)
+    def _(over):
+        send_packed(0, over)
+
+    @pl.loop(1, side)
+    def _(turn):
+        down = (side + near_first(turn)) % side
+        want_copy(side - down, (me_y + down) % side).wait_recv()
+        read_wants((me_y + down) % side)
+
+        @pl.loop(0, side)
+        def _(over):
+            send_packed(down, over)
 
     for slot in range(CAP):
         got[me_t * CAP + slot] = depths[wants_at[me_t, 0, me_t * CAP + slot]]
 
-    @pl.loop(0, tile_steps)
+    @pl.loop(1, tiles)
     def _(step):
-        to, source = tile_pair(step)
+        to, source = shifted(step // side, step % side)
         pack_copy(step, to, source).wait_recv()
 
     @pl.loop(0, own)
     def _(which):
-        @pl.loop(0, depth_steps)
-        def _(step):
-            to = depth_pair(step)[0]
+        @pl.loop(1, spread)
+        def _(turn):
+            step = spread - turn
+            to = peer(step)[0]
             chosen[which, to] = got[slot_at[0, to * own + which]]
             phase_copy(which, step, to, me_d).start()
 
@@ -255,9 +319,9 @@
     load_table.wait()
     load_pixels.wait()
 
-    @pl.loop(0, depth_steps)
+    @pl.loop(1, spread)
     def _(step):
-        to, source = depth_pair(step)
+        to, source = peer(step)
         pixel_copy(step, to, source).wait_recv()
 
     @pl.loop(0, own)
@@ -269,9 +333,9 @@
 
     @pl.loop(0, own)
     def _(which):
-        @pl.loop(0, depth_steps)
+        @pl.loop(1, spread)
         def _(step):
-            to, source = depth_pair(step)
+            to, source = peer(step)
             phase_copy(which, step, to, source).wait_recv()
 
         cosine, sine = cos_sin(phase[which])
@@ -287,30 +351,50 @@
         field_imag = both[:extent, extent:] + both[extent:, :extent]
         intensity[which] = field_real * field_real + field_imag * field_imag
 
-        @pl.loop(0, depth_steps)
-        def _(step):
-            out_copy(which, step, depth_pair(step)[0], me_d).start()
+        @pl.when(which < own - 1)
+        def _():
+            @pl.loop(1, spread)
+            def _(turn):
+                step = spread - turn
+                out_copy(which, step, peer(step)[0], me_d).start()
+
+        @pl.when(which == own - 1)
+        def _():
+            for low, high in zip(EDGES, EDGES[1:]):
+
+                @pl.loop(1, spread)
+                def _(turn):
+                    step = spread - turn
+                    to = peer(step)[0]
+
+                    @pl.when((to * 8 >= low * spread) & (to * 8 < high * spread))
+                    def _():
+                        out_copy(which, step, to, me_d).start()
 
         pltpu.make_async_copy(
             intensity.at[which, pl.ds(me_d * rows, rows), :], out.at[me_d * own + which], local_sem.at[4 + which]
         ).start()
 
-    @pl.loop(0, tile_steps)
+    @pl.loop(1, side)
+    def _(shift):
+        row_copy(shift, me_t).wait_send()
+        want_copy(shift, me_y).wait_send()
+
+    @pl.loop(1, tiles)
     def _(step):
-        to, source = tile_pair(step)
-        want_copy(step, to, source).wait_send()
+        to, source = shifted(step // side, step % side)
         pack_copy(step, to, source).wait_send()
 
-    @pl.loop(0, depth_steps)
+    @pl.loop(1, spread)
     def _(step):
-        to, source = depth_pair(step)
+        to, source = peer(step)
         pixel_copy(step, to, source).wait_send()
 
     @pl.loop(0, own)
     def _(which):
-        @pl.loop(0, depth_steps)
+        @pl.loop(1, spread)
         def _(step):
-            to, source = depth_pair(step)
+            to, source = peer(step)
             phase_copy(which, step, to, source).wait_send()
             out_copy(which, step, to, source).wait()
 
@@ -326,15 +410,16 @@
         count, rows, extent = patches.shape
         own = count // spread
         depth_count = phases.shape[0]
+        ring_rounds, side = reaches(spread)[1], math.isqrt(tiles)
         tables = jnp.asarray(dft_tables(extent))
         any_space = pl.BlockSpec(memory_space=pl.ANY)
         scalars = pl.BlockSpec(memory_space=pltpu.SMEM)
         f32, dma = jnp.float32, pltpu.SemaphoreType.DMA
         return pl.pallas_call(
             functools.partial(kernel, tiles),
-            out_shape=jax.ShapeDtypeStruct(patches.shape, patches.dtype),
+            out_shape=pltpu.VMEM(patches.shape, patches.dtype),
             in_specs=[any_space, scalars, scalars, any_space, any_space],
-            out_specs=any_space,
+            out_specs=pl.BlockSpec(memory_space=pltpu.VMEM),
             scratch_shapes=[
                 pltpu.VMEM(tables.shape, tables.dtype),
                 pltpu.VMEM((depth_count, rows, extent), f32),
@@ -350,9 +435,12 @@
                 pltpu.VMEM((own, extent, extent), f32),
                 pltpu.VMEM((own, 2, extent, extent), f32),
                 pltpu.VMEM((own, extent, extent), f32),
+                pltpu.SemaphoreType.REGULAR((ring_rounds, 2)),
                 dma((4 + own,)),
-                dma((tiles,)),
-                dma((tiles,)),
+                dma((side,)),
+                dma((side,)),
+                dma((side,)),
+                dma((side,)),
                 dma((tiles,)),
                 dma((tiles,)),
                 dma((spread,)),

time: 92.7 us -> 86.8 us (0.936)
  Pallas kernels: 90.6 us -> 85.1 us
  local copies, waits for them, and re-layouts: 1.87 us -> 0.8 us
    pallas_call x1, Pallas kernels: 90.6 us -> 85.1 us  [on_device(): pl.pallas_call(functools.partial(kernel, tiles), out_shape=pltpu.VMEM(pat...]
    unnamed x1, local copies, waits for them, and re-layouts: 1.87 us -> 0.8 us
where the time goes in v2:
time: 86.8 us; the launch traced here: 85.9 us
  Pallas kernels  85.1 us (98%)
    pallas_call x1, Pallas kernels, on_device(): pl.pallas_call(functools.partial(kernel, tiles), out_shape=pltpu.VMEM(pat...  85.1 us

profile of v2, /device:TPU:1, one launch (start us, length us, event | category | flops | bytes accessed | tf_op | source)
XLA Modules:
  0.0 85.9 jit_solution(3589505388356028450)
XLA Ops:
  0.0 85.1 %shard_map.55 = f32[64,8,256]{2,1,0:T(8,128)S(1)} custom-call(f32[64,8,256]{2,1,0:T(8,128)} %patches.1, s32[1,64]{1,0:T(1,128)} %bitcast.4, s32[1,64]{1,0:T(1,128)} %bitcast.5, f32[64,8,256]{2,1,0:T(8,128)} %bitcast.3, bf16[512,768]{1,0:T(8,128)(2,1)} %constant.2.clone.tables), custom_call_target="tpu_custom_call" | custom-call | tf_op jit(solution)/shard_map/pallas_call | solution.py:418
  85.1 0.8 copy.7

commit v3 on v2

--- a/solution.py
+++ b/solution.py
@@ -11,7 +11,7 @@
 
 CAP = 8
 LANES = 128
-EDGES = (0, 1, 2, 3, 4, 8)
+EDGES = (0, 1, 2, 3, 4, 5, 6, 7, 8)
 
 
 def dft_tables(extent):

time: 86.8 us -> 85.8 us (0.988)
  no operation moved by 1% of the time
where the time goes in v3:
time: 85.8 us; the launch traced here: 85.4 us
  Pallas kernels  84.6 us (99%)
    pallas_call x1, Pallas kernels, on_device(): pl.pallas_call(functools.partial(kernel, tiles), out_shape=pltpu.VMEM(pat...  84.6 us

profile of v3, /device:TPU:1, one launch (start us, length us, event | category | flops | bytes accessed | tf_op | source)
XLA Modules:
  0.0 85.4 jit_solution(1011762292454295358)
XLA Ops:
  0.0 84.6 %shard_map.55 = f32[64,8,256]{2,1,0:T(8,128)S(1)} custom-call(f32[64,8,256]{2,1,0:T(8,128)} %patches.1, s32[1,64]{1,0:T(1,128)} %bitcast.4, s32[1,64]{1,0:T(1,128)} %bitcast.5, f32[64,8,256]{2,1,0:T(8,128)} %bitcast.3, bf16[512,768]{1,0:T(8,128)(2,1)} %constant.2.clone.tables), custom_call_target="tpu_custom_call" | custom-call | tf_op jit(solution)/shard_map/pallas_call | solution.py:418
  84.6 0.8 copy.7

commit v4 on v3

--- a/solution.py
+++ b/solution.py
@@ -73,13 +73,16 @@
 def kernel(
     tiles,
     patches,
-    owner,
-    level,
+    owners_in,
+    levels_in,
     phases,
     tables,
     out,
     table,
+    held,
     depths,
+    owner,
+    level,
     slot_row,
     slot_at,
     want_row,
@@ -154,6 +157,12 @@
             tell_ring(turn + 1)
         send_pixels(turn + 1)
 
+    load_owner = pltpu.make_async_copy(owners_in, owner, local_sem.at[3])
+    load_owner.start()
+    load_level = pltpu.make_async_copy(levels_in, level, local_sem.at[4 + own])
+    load_level.start()
+    load_held = pltpu.make_async_copy(patches, held, local_sem.at[5 + own])
+    load_held.start()
     load_depths = pltpu.make_async_copy(phases, depths, local_sem.at[0])
     load_depths.start()
     load_table = pltpu.make_async_copy(tables, table, local_sem.at[1])
@@ -162,6 +171,9 @@
         patches.at[pl.ds(me_d * own, own)], pixels.at[:, pl.ds(me_d * rows, rows), :], local_sem.at[2]
     )
     load_pixels.start()
+
+    load_owner.wait()
+    load_level.wait()
 
     lane = lax.broadcasted_iota(jnp.int32, (1, LANES), 1)
     owners = lax.fori_loop(
@@ -209,7 +221,7 @@
 
     def pixel_copy(step, to, source):
         return pltpu.make_async_remote_copy(
-            src_ref=patches.at[pl.ds(to * own, own)],
+            src_ref=held.at[pl.ds(to * own, own)],
             dst_ref=pixels.at[:, pl.ds(source * rows, rows), :],
             send_sem=pixel_send.at[step],
             recv_sem=pixel_recv.at[step],
@@ -267,6 +279,7 @@
     def _(shift):
         row_copy(shift, me_t).start()
 
+    load_held.wait()
     send_pixels(0)
     learn_ring(0)
 
@@ -413,16 +426,18 @@
         ring_rounds, side = reaches(spread)[1], math.isqrt(tiles)
         tables = jnp.asarray(dft_tables(extent))
         any_space = pl.BlockSpec(memory_space=pl.ANY)
-        scalars = pl.BlockSpec(memory_space=pltpu.SMEM)
         f32, dma = jnp.float32, pltpu.SemaphoreType.DMA
         return pl.pallas_call(
             functools.partial(kernel, tiles),
             out_shape=pltpu.VMEM(patches.shape, patches.dtype),
-            in_specs=[any_space, scalars, scalars, any_space, any_space],
+            in_specs=[any_space] * 5,
             out_specs=pl.BlockSpec(memory_space=pltpu.VMEM),
             scratch_shapes=[
                 pltpu.VMEM(tables.shape, tables.dtype),
+                pltpu.VMEM(patches.shape, f32),
                 pltpu.VMEM((depth_count, rows, extent), f32),
+                pltpu.SMEM((1, count), jnp.int32),
+                pltpu.SMEM((1, count), jnp.int32),
                 pltpu.VMEM((1, LANES), jnp.int32),
                 pltpu.SMEM((1, LANES), jnp.int32),
                 pltpu.VMEM((1, LANES), jnp.int32),
@@ -436,7 +451,7 @@
                 pltpu.VMEM((own, 2, extent, extent), f32),
                 pltpu.VMEM((own, extent, extent), f32),
                 pltpu.SemaphoreType.REGULAR((ring_rounds, 2)),
-                dma((4 + own,)),
+                dma((6 + own,)),
                 dma((side,)),
                 dma((side,)),
                 dma((side,)),

time: 85.8 us -> 85.1 us (level)
  Pallas kernels: 84.6 us -> 83.5 us
    pallas_call x1, Pallas kernels: 84.6 us -> 83.5 us  [on_device(): pl.pallas_call(functools.partial(kernel, tiles), out_shape=pltpu.VMEM(pat...]
where the time goes in v4:
time: 85.1 us; the launch traced here: 84.3 us
  Pallas kernels  83.5 us (98%)
    pallas_call x1, Pallas kernels, on_device(): pl.pallas_call(functools.partial(kernel, tiles), out_shape=pltpu.VMEM(pat...  83.5 us

profile of v4, /device:TPU:1, one launch (start us, length us, event | category | flops | bytes accessed | tf_op | source)
XLA Modules:
  0.0 84.3 jit_solution(11793249201469137019)
XLA Ops:
  0.0 83.5 %shard_map.55 = f32[64,8,256]{2,1,0:T(8,128)S(1)} custom-call(f32[64,8,256]{2,1,0:T(8,128)} %patches.1, s32[1,64]{1,0:T(1,128)} %bitcast.4, s32[1,64]{1,0:T(1,128)} %bitcast.5, f32[64,8,256]{2,1,0:T(8,128)} %bitcast.3, bf16[512,768]{1,0:T(8,128)(2,1)} %constant.2.clone.tables), custom_call_target="tpu_custom_call" | custom-call | tf_op jit(solution)/shard_map/pallas_call | solution.py:430
  83.5 0.8 copy.7

commit v5 on v4

--- a/solution.py
+++ b/solution.py
@@ -138,7 +138,7 @@
 
     @pl.loop(1, within(reach))
     def _(step):
-        pl.semaphore_signal(barrier, inc=1, device_id={"depth": peer(step)[0]})
+        pl.semaphore_signal(barrier, inc=1, device_id={"depth": peer(within(reach) - step)[0]})
 
     @pl.loop(1, side)
     def _(shift):

time: 85.1 us -> 85 us (level)
  no operation moved by 1% of the time
where the time goes in v5:
time: 85 us; the launch traced here: 84.7 us
  Pallas kernels  83.9 us (99%)
    pallas_call x1, Pallas kernels, on_device(): pl.pallas_call(functools.partial(kernel, tiles), out_shape=pltpu.VMEM(pat...  83.9 us

profile of v5, /device:TPU:1, one launch (start us, length us, event | category | flops | bytes accessed | tf_op | source)
XLA Modules:
  0.0 84.7 jit_solution(18019251128355840376)
XLA Ops:
  0.0 83.9 %shard_map.55 = f32[64,8,256]{2,1,0:T(8,128)S(1)} custom-call(f32[64,8,256]{2,1,0:T(8,128)} %patches.1, s32[1,64]{1,0:T(1,128)} %bitcast.4, s32[1,64]{1,0:T(1,128)} %bitcast.5, f32[64,8,256]{2,1,0:T(8,128)} %bitcast.3, bf16[512,768]{1,0:T(8,128)(2,1)} %constant.2.clone.tables), custom_call_target="tpu_custom_call" | custom-call | tf_op jit(solution)/shard_map/pallas_call | solution.py:430
  83.9 0.8 copy.7
